TPU v7x, 256 devices: a whole 4x4x8 slice. The times are simulated.
256 devices in a mesh: atoms: 64 (over z_hi, y, x, core), gsplit: 4 (over z_lo).
Axes of the slice: x: 4, y: 4, z: 8 (z_hi: 2, z_lo: 4; z = z_hi * 4 + z_lo), core: 2. Of those that a mesh axis runs over, the one named last changes fastest.
Arguments:
- miller: int32 [3, 30720], P(None, 'gsplit'), may hold values from -16 to 16, as said below
- form_factors: bfloat16 [49, 30720], P(None, 'gsplit'), may hold values from -6 to 6
- fractional: float32 [3, 4096], P(None, 'atoms'), may hold values from 0 to 1
- multipoles: bfloat16 [2, 49, 4096], P(None, None, 'atoms'), may hold values from -0.013671875 to 0.013671875
- point_owner: int32 [8192], P(('atoms', 'gsplit')), may hold values from 0 to 63
- offsets: float32 [3, 8192], P(None, ('atoms', 'gsplit')), may hold values from -0.05 to 0.05
Outputs:
- grid_potential: float32 [2, 8192], P(None, ('atoms', 'gsplit'))
- moments: float32 [2, 49, 4096], P(None, None, ('atoms', 'gsplit'))
Inputs may be any that keep to these rules, and one draw needn't show every extreme that they name: `miller`: no vector has all three indices zero. Point p belongs to atom (p // 128) * 64 + point_owner[p].
All inputs are finite; a program needn't handle non-finite values.
Results may differ from a plain program's by a relative error of at most 0.0045.
Values may be sent and summed in bfloat16 or wider, within the bound.
No kernel may reach another device: no remote copies, remote signals or barrier semaphores. Data moves between devices by JAX's collectives and lax.ppermute only.
A program may use at most 64 MiB of HBM per device.

v0:
```python
import functools
import itertools

import jax
import jax.numpy as jnp
from jax import lax
from jax.experimental import pallas as pl
from jax.experimental.pallas import tpu as pltpu
from jax.sharding import Mesh
from jax.sharding import PartitionSpec as P


damping = 1.0 / 400.0
AXES = ("zh", "y", "x", "c", "g")
SIZES = {"zh": 2, "y": 4, "x": 4, "c": 2, "g": 4}
ROWS = 56

SIN = (4.442883014678955, -7.308245658874512, 3.606353998184204, -0.8461104035377502, 0.10982204228639603)
COS = (1.4142135381698608, -6.978850841522217, 5.73945951461792, -1.8835527896881104, 0.3106778562068939)


def exchanged(value, **flips):
    axes = tuple(axis for axis in AXES if axis in flips)
    sizes = [SIZES[axis] for axis in axes]
    pairs = []
    for place in itertools.product(*[range(size) for size in sizes]):
        other = [at ^ flips[axis] for at, axis in zip(place, axes)]
        flat = lambda spot: functools.reduce(lambda done, pair: done * pair[1] + pair[0], zip(spot, sizes), 0)
        pairs.append((flat(place), flat(other)))
    return lax.ppermute(value, axes, pairs)


def turns(columns, indices):
    angle = columns[0] * indices[0] + columns[1] * indices[1] + columns[2] * indices[2]
    rest = angle - jnp.round(angle)
    square = rest * rest
    sine = SIN[4]
    cosine = COS[4]
    for power in (3, 2, 1, 0):
        sine = sine * square + SIN[power]
        cosine = cosine * square + COS[power]
    sine = sine * rest
    return 1.0 - sine * sine, sine * cosine


def half_start(flip, width):
    half = lax.axis_index("c")
    if flip:
        half = 1 - half
    return half * width


def tables_into(table_ref, columns, miller_ref, base, start, count):
    vectors = miller_ref[:, pl.ds(pl.multiple_of(base + start, 128), 128)].astype(jnp.float32)
    indices = [vectors[axis : axis + 1, :] for axis in range(3)]
    for low in range(0, count, 64):
        part = [values[low : low + 64] for values in columns]
        cosine, sine = turns(part, indices)
        spot = pl.ds(pl.multiple_of(start, 128), 128)
        table_ref[low : low + 64, spot] = cosine.astype(jnp.bfloat16)
        table_ref[count + low : count + low + 64, spot] = sine.astype(jnp.bfloat16)


def row_signs(comps, lanes):
    rows = lax.broadcasted_iota(jnp.int32, (comps, lanes), 0)
    even = jnp.zeros((comps, lanes), jnp.float32)
    odd = jnp.zeros((comps, lanes), jnp.float32)
    degree = 0
    while degree * degree < comps:
        here = (rows >= degree * degree) & (rows < (degree + 1) * (degree + 1))
        sign = (1.0, -1.0, -1.0, 1.0)[degree % 4]
        if degree % 2 == 0:
            even = jnp.where(here, sign, even)
        else:
            odd = jnp.where(here, sign, odd)
        degree += 1
    return even, odd


def structure_into(base, columns, lhs, miller_ref, form_ref, table_ref, sums_ref, form_ready):
    width = table_ref.shape[1]
    comps = form_ref.shape[0]
    for start in range(0, width, 256):
        cosines, sines = [], []
        for part in range(2):
            there = pl.ds(pl.multiple_of(base + start + 128 * part, 128), 128)
            vectors = miller_ref[:, there].astype(jnp.float32)
            cosine, sine = turns(columns, [vectors[axis : axis + 1, :] for axis in range(3)])
            cosines.append(cosine.astype(jnp.bfloat16))
            sines.append(sine.astype(jnp.bfloat16))
        table = jnp.concatenate([jnp.concatenate(cosines, axis=1), jnp.concatenate(sines, axis=1)], axis=0)
        table_ref[:, start : start + 256] = table
        along = jnp.dot(lhs, table, preferred_element_type=jnp.float32)
        if start == 0:
            form_ready()
        form = form_ref[:, pl.ds(pl.multiple_of(base + start, 128), 256)].astype(jnp.float32)
        for row in range(4):
            part = along[ROWS * row : ROWS * row + comps]
            sums_ref[row : row + 1, start : start + 256] = jnp.sum(form * part, axis=0, keepdims=True)


def first_kernel(
    miller_hbm, form_hbm, frac_hbm, poles_hbm, owner_hbm, offsets_hbm,
    table_ref, sums_ref, places_ref, miller_ref, form_ref, lhs_ref, frac_ref,
    frac_in, poles_ref, owner_ref, offsets_ref, lhs_scr, sems,
):
    width = table_ref.shape[1]
    comps = form_ref.shape[0]
    atoms = frac_in.shape[1]
    base = half_start(True, width)
    other = half_start(False, width)
    far = pl.ds(pl.multiple_of(base, 128), width)
    near = pl.ds(pl.multiple_of(other, 128), width)
    moves = [
        (frac_hbm, frac_in),
        (poles_hbm, poles_ref),
        (miller_hbm, miller_ref),
        (form_hbm.at[:, far], form_ref.at[:, far]),
        (owner_hbm, owner_ref),
        (offsets_hbm, offsets_ref),
        (form_hbm.at[:, near], form_ref.at[:, near]),
    ]
    copies = [pltpu.make_async_copy(start, end, sems.at[spot]) for spot, (start, end) in enumerate(moves)]
    for copy in copies:
        copy.start()
    frac_ref[...] = jnp.zeros_like(frac_ref)
    lhs_scr[...] = jnp.zeros_like(lhs_scr)
    places_ref[...] = jnp.zeros_like(places_ref)
    even, odd = row_signs(comps, atoms)
    copies[0].wait()
    frac_ref[0:3, 0:atoms] = frac_in[...]
    turned = frac_ref[...].T
    columns = [turned[0:atoms, axis : axis + 1] for axis in range(3)]
    copies[1].wait()
    for density in range(2):
        poles = poles_ref[:, density, :].astype(jnp.float32)
        low = 2 * ROWS * density
        lhs_scr[low : low + comps, :] = jnp.concatenate([poles * even, poles * odd], axis=1)
        lhs_scr[low + ROWS : low + ROWS + comps, :] = jnp.concatenate([poles * odd, -(poles * even)], axis=1)
    lhs = lhs_scr[...].astype(jnp.bfloat16)
    lhs_ref[...] = lhs
    copies[2].wait()
    structure_into(base, columns, lhs, miller_ref, form_ref, table_ref, sums_ref, copies[3].wait)
    copies[4].wait()
    copies[5].wait()
    points = owner_ref.shape[1]
    chosen = lax.broadcasted_iota(jnp.int32, (atoms, points), 0) == owner_ref[...]
    for axis in range(3):
        spread = jnp.where(chosen, columns[axis], 0.0)
        places_ref[axis : axis + 1, :] = jnp.sum(spread, axis=0, keepdims=True) + offsets_ref[axis : axis + 1, :]
    copies[6].wait()


def second_kernel(miller_ref, form_ref, lhs_ref, frac_ref, table_ref, sums_ref):
    atoms = table_ref.shape[0] // 2
    base = half_start(False, table_ref.shape[1])
    turned = frac_ref[...].T
    columns = [turned[0:atoms, axis : axis + 1] for axis in range(3)]
    structure_into(base, columns, lhs_ref[...], miller_ref, form_ref, table_ref, sums_ref, lambda: None)


def points_kernel(flip, miller_ref, places_ref, table_ref):
    width = table_ref.shape[1]
    base = half_start(flip, width)
    turned = places_ref[...].T
    columns = [turned[:, axis : axis + 1] for axis in range(3)]
    count = turned.shape[0]
    unroll = 5

    def step(index, carry):
        for inner in range(unroll):
            tables_into(table_ref, columns, miller_ref, base, (index * unroll + inner) * 128, count)
        return carry

    lax.fori_loop(0, width // (128 * unroll), step, 0)


def moments_kernel(flip, comps, *refs):
    miller_ref, form_ref, sums_ref, atoms_ref, points_ref = refs[:5]
    if flip:
        before_ref, refs = refs[5], refs[6:]
        outs, (form_scr, cos_scr, sin_scr, turned_scr) = refs[:4], refs[4:]
    else:
        out_ref, form_scr, cos_scr, sin_scr = refs[5:]
    width = atoms_ref.shape[1]
    base = half_start(flip, width)
    rows = lax.broadcasted_iota(jnp.int32, (ROWS, 128), 0)
    even = rows == comps
    for degree in range(0, 16, 2):
        even = even | ((rows >= degree * degree) & (rows < min((degree + 1) * (degree + 1), comps)))
    ones = (lax.broadcasted_iota(jnp.int32, (ROWS - comps, 128), 0) == 0).astype(jnp.float32)
    atoms = atoms_ref.shape[0] // 2
    points = points_ref.shape[0] // 2
    contract = (((1,), (1,)), ((), ()))
    total = before_ref[...] if flip else None
    chunk = width // 3
    for slot in range(form_scr.shape[0]):
        form_scr[slot, comps:ROWS, :] = ones
    for first in range(0, width, chunk):
        for start in range(first, first + chunk, 128):
            there = pl.ds(pl.multiple_of(base + start, 128), 128)
            vectors = miller_ref[:, there].astype(jnp.float32)
            square = jnp.sum(vectors * vectors, axis=0, keepdims=True)
            kernel = jnp.exp(-damping * square) / square
            potential = kernel * sums_ref[:, start : start + 128]
            slot = (start // 128) % form_scr.shape[0]
            form_scr[slot, 0:comps, :] = form_ref[:, there].astype(jnp.float32)
            form = form_scr[slot]
            against_cos, against_sin = [], []
            for density in range(2):
                real = potential[2 * density : 2 * density + 1]
                imag = potential[2 * density + 1 : 2 * density + 2]
                against_cos.append(form * jnp.where(even, real, imag))
                against_sin.append(form * jnp.where(even, -imag, real))
            cos_scr[:, start : start + 128] = jnp.concatenate(against_cos, axis=0).astype(jnp.bfloat16)
            sin_scr[:, start : start + 128] = jnp.concatenate(against_sin, axis=0).astype(jnp.bfloat16)
        span = slice(first, first + chunk)
        for part, weights in enumerate((cos_scr, sin_scr)):
            table = jnp.concatenate(
                [
                    atoms_ref[atoms * part : atoms * (part + 1), span],
                    points_ref[points * part : points * (part + 1), span],
                ],
                axis=0,
            )
            term = lax.dot_general(weights[:, span], table, contract, preferred_element_type=jnp.float32)
            total = term if total is None else total + term
    if not flip:
        out_ref[...] = total
        return
    pad = jnp.zeros((2 * ROWS, turned_scr.shape[0] - atoms - points), jnp.float32)
    turned_scr[...] = jnp.concatenate([total, pad], axis=1).T
    own = lax.axis_index("g")
    for turn, out_ref in enumerate(outs):
        few = atoms // 4
        many = points // 4
        out_ref[0:few] = turned_scr[pl.ds(pl.multiple_of((own ^ turn) * few, few), few)]
        out_ref[few : few + many] = turned_scr[atoms + many * turn : atoms + many * (turn + 1)]


def finish_kernel(comps, atoms, first_ref, second_ref, third_ref, fourth_ref, grid_ref, moments_ref):
    total = (first_ref[...] + second_ref[...]) + (third_ref[...] + fourth_ref[...])
    turned = total.T
    place = lax.broadcasted_iota(jnp.int32, (atoms, comps), 1)
    sign = jnp.zeros((atoms, comps), jnp.float32)
    degree = 0
    while degree * degree < comps:
        here = (place >= degree * degree) & (place < (degree + 1) * (degree + 1))
        sign = jnp.where(here, (1.0, -1.0, -1.0, 1.0)[degree % 4], sign)
        degree += 1
    for density in range(2):
        low = ROWS * density
        moments_ref[density] = total[0:atoms, low : low + comps] * sign
        grid_ref[density : density + 1, :] = turned[low + comps : low + comps + 1, atoms:]


def cost(flops):
    return pl.CostEstimate(flops=flops, bytes_accessed=1 << 20, transcendentals=0)


PARAMS = pltpu.CompilerParams(vmem_limit_bytes=24 << 20)


def shards(miller, form_factors, fractional, multipoles, point_owner, offsets):
    comps, vectors = form_factors.shape
    atoms = fractional.shape[1]
    half = vectors // 2
    own_points = offsets.shape[1]
    points = 4 * own_points
    few = atoms // 4
    shape = jax.ShapeDtypeStruct

    table_shapes = (shape((2 * atoms, half), jnp.bfloat16), shape((4, half), jnp.float32))
    structure_cost = cost(2 * half * 128 * 224 * 8)
    far_table, far_sums, places, miller, form_factors, lhs, frac = pl.pallas_call(
        first_kernel,
        in_specs=[pl.BlockSpec(memory_space=pltpu.HBM)] * 6,
        out_shape=(
            *table_shapes,
            shape((8, own_points), jnp.float32),
            shape(miller.shape, miller.dtype),
            shape(form_factors.shape, form_factors.dtype),
            shape((4 * ROWS, 2 * atoms), jnp.bfloat16),
            shape((8, 128), jnp.float32),
        ),
        scratch_shapes=[
            pltpu.VMEM((3, atoms), jnp.float32),
            pltpu.VMEM((comps, 2, atoms), jnp.bfloat16),
            pltpu.VMEM((1, own_points), jnp.int32),
            pltpu.VMEM((3, own_points), jnp.float32),
            pltpu.VMEM((4 * ROWS, 2 * atoms), jnp.float32),
            pltpu.SemaphoreType.DMA((7,)),
        ],
        compiler_params=PARAMS,
        cost_estimate=structure_cost,
        name="structure1",
    )(
        *[
            pltpu.with_memory_space_constraint(value, pltpu.HBM)
            for value in (
                miller, form_factors, fractional, jnp.transpose(multipoles, (1, 0, 2)), point_owner[None], offsets
            )
        ]
    )

    arrived = exchanged(far_sums, c=1)
    places = jnp.concatenate([places, exchanged(places, g=1)], axis=1)
    near_table, near_sums = pl.pallas_call(
        second_kernel,
        out_shape=table_shapes,
        compiler_params=PARAMS,
        cost_estimate=structure_cost,
        name="structure0",
    )(miller, form_factors, lhs, frac)
    sums = near_sums + arrived
    sums, places = lax.optimization_barrier((sums, places))

    def point_table(flip):
        return pl.pallas_call(
            functools.partial(points_kernel, flip),
            out_shape=shape((2 * points, half), jnp.bfloat16),
            compiler_params=PARAMS,
            cost_estimate=cost(2 * half * 128 * 224 * 8),
        )(miller, places)

    crossed = exchanged(sums, zh=1)
    others = exchanged(places, g=2)
    places = jnp.concatenate([places, others], axis=1)
    sums = sums + crossed
    far_points = point_table(1)
    near_points = point_table(0)
    for stage in (
        [dict(y=1, x=1), dict(x=1), dict(y=1)],
        [dict(y=3, x=3), dict(x=3), dict(y=3)],
    ):
        parts = [exchanged(sums, **flips) for flips in stage]
        for part in parts:
            sums = sums + part
    other_sums = exchanged(sums, c=1)

    def contract(flip, summed, atom_table, point_rows, before):
        if flip:
            out_shape = [shape((few + own_points, 2 * ROWS), jnp.float32)] * 4
            more = [pltpu.VMEM((256, 2 * ROWS), jnp.float32)]
        else:
            out_shape = shape((2 * ROWS, atoms + points), jnp.float32)
            more = []
        return pl.pallas_call(
            functools.partial(moments_kernel, flip, comps),
            out_shape=out_shape,
            scratch_shapes=[
                pltpu.VMEM((5, ROWS, 128), jnp.float32),
                pltpu.VMEM((2 * ROWS, half), jnp.bfloat16),
                pltpu.VMEM((2 * ROWS, half), jnp.bfloat16),
                *more,
            ],
            compiler_params=PARAMS,
            cost_estimate=cost(2 * half * 256 * 112 * 8),
        )(miller, form_factors, summed, atom_table, point_rows, *before)

    near = contract(0, sums, near_table, near_points, ())
    pieces = contract(1, other_sums, far_table, far_points, (near,))
    pieces = [pieces[0]] + [exchanged(pieces[turn], g=turn) for turn in (1, 2, 3)]
    grid, moments = pl.pallas_call(
        functools.partial(finish_kernel, comps, few),
        out_shape=[shape((2, own_points), jnp.float32), shape((2, few, comps), jnp.float32)],
        compiler_params=PARAMS,
        cost_estimate=cost(1 << 20),
        name="finish",
    )(*pieces)
    return grid, jnp.transpose(moments, (0, 2, 1))


def solution(mesh):
    fine = Mesh(mesh.devices.reshape([SIZES[axis] for axis in AXES]), AXES)
    block = ("zh", "y", "x", "c")
    placed = (
        P(None, "g"),
        P(None, "g"),
        P(None, block),
        P(None, None, block),
        P(AXES),
        P(None, AXES),
    )
    return jax.shard_map(
        shards,
        mesh=fine,
        in_specs=placed,
        out_specs=(P(None, AXES), P(None, None, AXES)),
        check_vma=False,
    )
```

profile of v0, /device:TPU:1, one launch (start us, length us, event | category | flops | bytes accessed | tf_op | source)
XLA Modules:
  0.0 50.5 jit_solution(2522638427198445082)
XLA Ops:
  0.6 2.9 %structure1.1 = (bf16[128,3840]{1,0:T(8,128)(2,1)S(1)}, f32[4,3840]{1,0:T(4,128)S(1)}, f32[8,32]{1,0:T(8,128)S(1)}, s32[3,7680]{1,0:T(4,128)S(1)}, bf16[49,7680]...) custom-call(s32[3,7680]{1,0:T(4,128)} %miller_hbm.1, bf16[49,7680]{1,0:T(8,128)(2,1)} %form_hbm.1, ...), custom_call_target="tpu_custom_call" | custom-call | flops 1761607680 | bytes 1048576 | tf_op jit(solution)/shard_map/structure1/pallas_call | solution.py:275
  3.5 2.5 %collective-permute-start.1 = (f32[8,32]{1,0:T(8,128)S(1)}, f32[8,32]{1,0:T(8,128)S(1)}, u32[]{:S(2)}, u32[]{:S(2)}) collective-permute-start(f32[8,32]{1,0:T(8,128)S(1)} %get-tuple-element.25), channel_id=1, source_target_pairs={{0,1},{1,0},{2,3},{3,2},{4,5},{5,4},{6,7},{7,6},{8,9},{9,8},{10,11... | collective-permute-start | bytes 3080 | tf_op jit(solution)/shard_map/ppermute | solution.py:30
  6.0 1.0 %collective-permute-start = (f32[4,3840]{1,0:T(4,128)S(1)}, f32[4,3840]{1,0:T(4,128)S(1)}, u32[]{:S(2)}, u32[]{:S(2)}) collective-permute-start(f32[4,3840]{1,0:T(4,128)S(1)} %get-tuple-element.24), channel_id=1, source_target_pairs={{0,4},{4,0},{1,5},{5,1},{2,6},{6,2},{3,7},{7,3},{8,12},{12,8},{9,1... | collective-permute-start | bytes 184328 | tf_op jit(solution)/shard_map/ppermute | solution.py:30
  7.0 1.7 %structure0.1 = (bf16[128,3840]{1,0:T(8,128)(2,1)S(1)}, f32[4,3840]{1,0:T(4,128)S(1)}) custom-call(s32[3,7680]{1,0:T(4,128)S(1)} %get-tuple-element.19.miller_ref.refs_0_, bf16[49,7680]{1,0:T(8,128)(2,1)S(1)} %get-tuple-element.20.form_ref.refs_1_, bf16[224,128]{1,0:T(8,128)(2,1)S(1)} %get-tuple-element.21.lhs_ref, f32[8,128]{1,0:T(8,128)S(1)} %get-tuple-element.22.frac_ref), custom_call_target="tpu_custom_call" | custom-call | flops 1761607680 | bytes 1048576 | tf_op jit(solution)/shard_map/structure0/pallas_call | solution.py:308
  8.7 0.0 collective-permute-done.1
  8.7 0.1 pad_maximum_fusion
  8.8 0.0 collective-permute-done
  8.8 3.1 %collective-permute-start.10 = (f32[8,64]{1,0:T(8,128)S(1)}, f32[8,64]{1,0:T(8,128)S(1)}, u32[]{:S(2)}, u32[]{:S(2)}) collective-permute-start(f32[8,64]{1,0:T(8,128)S(1)} %pad_maximum_fusion), channel_id=1, source_target_pairs={{0,2},{1,3},{2,0},{3,1},{4,6},{5,7},{6,4},{7,5},{8,10},{9,11},{10,... | collective-permute-start | bytes 6152 | tf_op jit(solution)/shard_map/ppermute | solution.py:30
  11.9 4.2 %collective-permute-start.2 = (f32[4,3840]{1,0:T(4,128)S(1)}, f32[4,3840]{1,0:T(4,128)S(1)}, u32[]{:S(2)}, u32[]{:S(2)}) collective-permute-start(f32[4,3840]{1,0:T(4,128)S(1)} %add.24), channel_id=1, source_target_pairs={{0,128},{128,0},{1,129},{129,1},{2,130},{130,2},{3,131},{131,3},{4... | collective-permute-start | bytes 184328 | tf_op jit(solution)/shard_map/ppermute | solution.py:30
  16.1 0.0 collective-permute-done.10
  16.1 0.1 pad_maximum_fusion.1.places_ref
  16.2 2.7 %collective-permute-done.2 = f32[4,3840]{1,0:T(4,128)S(1)} collective-permute-done((f32[4,3840]{1,0:T(4,128)S(1)}, f32[4,3840]{1,0:T(4,128)S(1)}, u32[]{:S(2)}, u32[]{:S(2)}) %collective-permute-start.2) | collective-permute-done | bytes 61472 | tf_op jit(solution)/shard_map/ppermute | solution.py:30
  19.0 1.4 %collective-permute-start.5 = (f32[4,3840]{1,0:T(4,128)S(1)}, f32[4,3840]{1,0:T(4,128)S(1)}, u32[]{:S(2)}, u32[]{:S(2)}) collective-permute-start(f32[4,3840]{1,0:T(4,128)S(1)} %add.25), channel_id=1, source_target_pairs={{0,32},{32,0},{64,96},{96,64},{1,33},{33,1},{65,97},{97,65},{2,34}... | collective-permute-start | bytes 184328 | tf_op jit(solution)/shard_map/ppermute | solution.py:30
  20.4 1.2 %collective-permute-start.4 = (f32[4,3840]{1,0:T(4,128)S(1)}, f32[4,3840]{1,0:T(4,128)S(1)}, u32[]{:S(2)}, u32[]{:S(2)}) collective-permute-start(f32[4,3840]{1,0:T(4,128)S(1)} %add.25), channel_id=1, source_target_pairs={{0,8},{8,0},{16,24},{24,16},{1,9},{9,1},{17,25},{25,17},{2,10},{10... | collective-permute-start | bytes 184328 | tf_op jit(solution)/shard_map/ppermute | solution.py:30
  21.6 0.1 collective-permute-start.3
  21.7 2.6 %shard_map.78.refs_4_ = bf16[256,3840]{1,0:T(8,128)(2,1)S(1)} custom-call(s32[3,7680]{1,0:T(4,128)S(1)} %get-tuple-element.19.miller_ref.refs_0_, f32[8,128]{1,0:T(8,128)S(1)} %pad_maximum_fusion.1.places_ref), custom_call_target="tpu_custom_call" | custom-call | flops 1761607680 | bytes 1048576 | tf_op jit(solution)/shard_map/pallas_call | solution.py:319
  24.3 0.0 collective-permute-done.5
  24.3 0.0 collective-permute-done.4
  24.3 1.8 %collective-permute-done.3 = f32[4,3840]{1,0:T(4,128)S(1)} collective-permute-done((f32[4,3840]{1,0:T(4,128)S(1)}, f32[4,3840]{1,0:T(4,128)S(1)}, u32[]{:S(2)}, u32[]{:S(2)}) %collective-permute-start.3) | collective-permute-done | bytes 61472 | tf_op jit(solution)/shard_map/ppermute | solution.py:30
  26.1 1.4 %collective-permute-start.8 = (f32[4,3840]{1,0:T(4,128)S(1)}, f32[4,3840]{1,0:T(4,128)S(1)}, u32[]{:S(2)}, u32[]{:S(2)}) collective-permute-start(f32[4,3840]{1,0:T(4,128)S(1)} %add_add_fusion.1), channel_id=1, source_target_pairs={{0,96},{32,64},{64,32},{96,0},{1,97},{33,65},{65,33},{97,1},{2,98}... | collective-permute-start | bytes 184328 | tf_op jit(solution)/shard_map/ppermute | solution.py:30
  27.6 2.1 %collective-permute-start.7 = (f32[4,3840]{1,0:T(4,128)S(1)}, f32[4,3840]{1,0:T(4,128)S(1)}, u32[]{:S(2)}, u32[]{:S(2)}) collective-permute-start(f32[4,3840]{1,0:T(4,128)S(1)} %add_add_fusion.1), channel_id=1, source_target_pairs={{0,24},{8,16},{16,8},{24,0},{1,25},{9,17},{17,9},{25,1},{2,26},{10... | collective-permute-start | bytes 184328 | tf_op jit(solution)/shard_map/ppermute | solution.py:30
  29.7 1.6 %collective-permute-start.6 = (f32[4,3840]{1,0:T(4,128)S(1)}, f32[4,3840]{1,0:T(4,128)S(1)}, u32[]{:S(2)}, u32[]{:S(2)}) collective-permute-start(f32[4,3840]{1,0:T(4,128)S(1)} %add_add_fusion.1), channel_id=1, source_target_pairs={{0,120},{8,112},{16,104},{24,96},{32,88},{40,80},{48,72},{56,64},{... | collective-permute-start | bytes 184328 | tf_op jit(solution)/shard_map/ppermute | solution.py:30
  31.3 2.6 %shard_map.77.refs_4_ = bf16[256,3840]{1,0:T(8,128)(2,1)S(1)} custom-call(s32[3,7680]{1,0:T(4,128)S(1)} %get-tuple-element.19.miller_ref.refs_0_, f32[8,128]{1,0:T(8,128)S(1)} %pad_maximum_fusion.1.places_ref), custom_call_target="tpu_custom_call" | custom-call | flops 1761607680 | bytes 1048576 | tf_op jit(solution)/shard_map/pallas_call | solution.py:319
  33.9 0.0 collective-permute-done.8
  33.9 0.0 collective-permute-done.7
  33.9 2.7 %collective-permute-done.6 = f32[4,3840]{1,0:T(4,128)S(1)} collective-permute-done((f32[4,3840]{1,0:T(4,128)S(1)}, f32[4,3840]{1,0:T(4,128)S(1)}, u32[]{:S(2)}, u32[]{:S(2)}) %collective-permute-start.6) | collective-permute-done | bytes 61472 | tf_op jit(solution)/shard_map/ppermute | solution.py:30
  36.6 4.1 %collective-permute-start.9 = (f32[4,3840]{1,0:T(4,128)S(1)}, f32[4,3840]{1,0:T(4,128)S(1)}, u32[]{:S(2)}, u32[]{:S(2)}) collective-permute-start(f32[4,3840]{1,0:T(4,128)S(1)} %add_add_fusion.refs_2_), channel_id=1, source_target_pairs={{0,4},{4,0},{1,5},{5,1},{2,6},{6,2},{3,7},{7,3},{8,12},{12,8},{9,1... | collective-permute-start | bytes 184328 | tf_op jit(solution)/shard_map/ppermute | solution.py:30
  40.7 1.2 %shard_map.79.refs_5_ = f32[112,192]{1,0:T(8,128)S(1)} custom-call(s32[3,7680]{1,0:T(4,128)S(1)} %get-tuple-element.19.miller_ref.refs_0_, bf16[49,7680]{1,0:T(8,128)(2,1)S(1)} %get-tuple-element.20.form_ref.refs_1_, f32[4,3840]{1,0:T(4,128)S(1)} %add_add_fusion.refs_2_, bf16[128,3840]{1,0:T(8,128)(2,1)S(1)} %get-tuple-element.29.refs_3_, ...), custom_call_target="tpu_custom_call" | custom-call | flops 1761607680 | bytes 1048576 | tf_op jit(solution)/shard_map/pallas_call | solution.py:348
  42.0 0.0 collective-permute-done.9.refs_2_
  42.0 1.4 %shard_map.80 = (f32[48,112]{1,0:T(8,128)S(1)}, f32[48,112]{1,0:T(8,128)S(1)}, f32[48,112]{1,0:T(8,128)S(1)}, f32[48,112]{1,0:T(8,128)S(1)}) custom-call(s32[3,7680]{1,0:T(4,128)S(1)} %get-tuple-element.19.miller_ref.refs_0_, bf16[49,7680]{1,0:T(8,128)(2,1)S(1)} %get-tuple-element.20.form_ref.refs_1_, f32[4,3840]{1,0:T(4,128)S(1)} %collective-permute-done.9.refs_2_, ...), custom_call_target="tpu_custom_call" | custom-call | flops 1761607680 | bytes 1048576 | tf_op jit(solution)/shard_map/pallas_call | solution.py:348
  43.3 2.0 %collective-permute-start.11 = (f32[48,112]{1,0:T(8,128)S(1)}, f32[48,112]{1,0:T(8,128)S(1)}, u32[]{:S(2)}, u32[]{:S(2)}) collective-permute-start(f32[48,112]{1,0:T(8,128)S(1)} %get-tuple-element.31), channel_id=1, source_target_pairs={{0,1},{1,0},{2,3},{3,2},{4,5},{5,4},{6,7},{7,6},{8,9},{9,8},{10,11... | collective-permute-start | bytes 64520 | tf_op jit(solution)/shard_map/ppermute | solution.py:30
  45.3 0.0 collective-permute-start.12
  45.3 2.2 %collective-permute-start.13 = (f32[48,112]{1,0:T(8,128)S(1)}, f32[48,112]{1,0:T(8,128)S(1)}, u32[]{:S(2)}, u32[]{:S(2)}) collective-permute-start(f32[48,112]{1,0:T(8,128)S(1)} %get-tuple-element.33), channel_id=1, source_target_pairs={{0,3},{1,2},{2,1},{3,0},{4,7},{5,6},{6,5},{7,4},{8,11},{9,10},{10,... | collective-permute-start | bytes 64520 | tf_op jit(solution)/shard_map/ppermute | solution.py:30
  47.5 0.0 collective-permute-done.11.second_ref
  47.5 1.7 %collective-permute-done.12.third_ref = f32[48,112]{1,0:T(8,128)S(1)} collective-permute-done((f32[48,112]{1,0:T(8,128)S(1)}, f32[48,112]{1,0:T(8,128)S(1)}, u32[]{:S(2)}, u32[]{:S(2)}) %collective-permute-start.12) | collective-permute-done | bytes 21536 | tf_op jit(solution)/shard_map/ppermute | solution.py:30
  49.2 0.6 %collective-permute-done.13.fourth_ref = f32[48,112]{1,0:T(8,128)S(1)} collective-permute-done((f32[48,112]{1,0:T(8,128)S(1)}, f32[48,112]{1,0:T(8,128)S(1)}, u32[]{:S(2)}, u32[]{:S(2)}) %collective-permute-start.13) | collective-permute-done | bytes 21536 | tf_op jit(solution)/shard_map/ppermute | solution.py:30
  49.8 0.8 %finish.1 = (f32[2,32]{1,0:T(2,128)}, f32[2,16,49]{2,1,0:T(8,128)}) custom-call(f32[48,112]{1,0:T(8,128)S(1)} %get-tuple-element.30.first_ref, f32[48,112]{1,0:T(8,128)S(1)} %collective-permute-done.11.second_ref, f32[48,112]{1,0:T(8,128)S(1)} %collective-permute-done.12.third_ref, f32[48,112]{1,0:T(8,128)S(1)} %collective-permute-done.13.fourth_ref), custom_call_target="tpu_custom_call" | custom-call | flops 1048576 | bytes 1048576 | tf_op jit(solution)/shard_map/finish/pallas_call | solution.py:364
  (4 shorter events, 0.1 us)
Async XLA Ops:
  3.5 5.2 %collective-permute-start.1 = (f32[8,32]{1,0:T(8,128)S(1)}, f32[8,32]{1,0:T(8,128)S(1)}, u32[]{:S(2)}, u32[]{:S(2)}) collective-permute-start(f32[8,32]{1,0:T(8,128)S(1)} %get-tuple-element.25), channel_id=1, source_target_pairs={{0,1},{1,0},{2,3},{3,2},{4,5},{5,4},{6,7},{7,6},{8,9},{9,8},{10,11... | collective-permute-start | bytes 3080 | tf_op jit(solution)/shard_map/ppermute | solution.py:30
  6.0 2.8 %collective-permute-start = (f32[4,3840]{1,0:T(4,128)S(1)}, f32[4,3840]{1,0:T(4,128)S(1)}, u32[]{:S(2)}, u32[]{:S(2)}) collective-permute-start(f32[4,3840]{1,0:T(4,128)S(1)} %get-tuple-element.24), channel_id=1, source_target_pairs={{0,4},{4,0},{1,5},{5,1},{2,6},{6,2},{3,7},{7,3},{8,12},{12,8},{9,1... | collective-permute-start | bytes 184328 | tf_op jit(solution)/shard_map/ppermute | solution.py:30
  8.8 7.3 %collective-permute-start.10 = (f32[8,64]{1,0:T(8,128)S(1)}, f32[8,64]{1,0:T(8,128)S(1)}, u32[]{:S(2)}, u32[]{:S(2)}) collective-permute-start(f32[8,64]{1,0:T(8,128)S(1)} %pad_maximum_fusion), channel_id=1, source_target_pairs={{0,2},{1,3},{2,0},{3,1},{4,6},{5,7},{6,4},{7,5},{8,10},{9,11},{10,... | collective-permute-start | bytes 6152 | tf_op jit(solution)/shard_map/ppermute | solution.py:30
  11.9 7.0 %collective-permute-start.2 = (f32[4,3840]{1,0:T(4,128)S(1)}, f32[4,3840]{1,0:T(4,128)S(1)}, u32[]{:S(2)}, u32[]{:S(2)}) collective-permute-start(f32[4,3840]{1,0:T(4,128)S(1)} %add.24), channel_id=1, source_target_pairs={{0,128},{128,0},{1,129},{129,1},{2,130},{130,2},{3,131},{131,3},{4... | collective-permute-start | bytes 184328 | tf_op jit(solution)/shard_map/ppermute | solution.py:30
  19.0 5.3 %collective-permute-start.5 = (f32[4,3840]{1,0:T(4,128)S(1)}, f32[4,3840]{1,0:T(4,128)S(1)}, u32[]{:S(2)}, u32[]{:S(2)}) collective-permute-start(f32[4,3840]{1,0:T(4,128)S(1)} %add.25), channel_id=1, source_target_pairs={{0,32},{32,0},{64,96},{96,64},{1,33},{33,1},{65,97},{97,65},{2,34}... | collective-permute-start | bytes 184328 | tf_op jit(solution)/shard_map/ppermute | solution.py:30
  20.4 4.0 %collective-permute-start.4 = (f32[4,3840]{1,0:T(4,128)S(1)}, f32[4,3840]{1,0:T(4,128)S(1)}, u32[]{:S(2)}, u32[]{:S(2)}) collective-permute-start(f32[4,3840]{1,0:T(4,128)S(1)} %add.25), channel_id=1, source_target_pairs={{0,8},{8,0},{16,24},{24,16},{1,9},{9,1},{17,25},{25,17},{2,10},{10... | collective-permute-start | bytes 184328 | tf_op jit(solution)/shard_map/ppermute | solution.py:30
  21.6 4.5 %collective-permute-start.3 = (f32[4,3840]{1,0:T(4,128)S(1)}, f32[4,3840]{1,0:T(4,128)S(1)}, u32[]{:S(2)}, u32[]{:S(2)}) collective-permute-start(f32[4,3840]{1,0:T(4,128)S(1)} %add.25), channel_id=1, source_target_pairs={{0,40},{8,32},{16,56},{24,48},{32,8},{40,0},{48,24},{56,16},{64,10... | collective-permute-start | bytes 184328 | tf_op jit(solution)/shard_map/ppermute | solution.py:30
  26.1 7.7 %collective-permute-start.8 = (f32[4,3840]{1,0:T(4,128)S(1)}, f32[4,3840]{1,0:T(4,128)S(1)}, u32[]{:S(2)}, u32[]{:S(2)}) collective-permute-start(f32[4,3840]{1,0:T(4,128)S(1)} %add_add_fusion.1), channel_id=1, source_target_pairs={{0,96},{32,64},{64,32},{96,0},{1,97},{33,65},{65,33},{97,1},{2,98}... | collective-permute-start | bytes 184328 | tf_op jit(solution)/shard_map/ppermute | solution.py:30
  27.6 6.3 %collective-permute-start.7 = (f32[4,3840]{1,0:T(4,128)S(1)}, f32[4,3840]{1,0:T(4,128)S(1)}, u32[]{:S(2)}, u32[]{:S(2)}) collective-permute-start(f32[4,3840]{1,0:T(4,128)S(1)} %add_add_fusion.1), channel_id=1, source_target_pairs={{0,24},{8,16},{16,8},{24,0},{1,25},{9,17},{17,9},{25,1},{2,26},{10... | collective-permute-start | bytes 184328 | tf_op jit(solution)/shard_map/ppermute | solution.py:30
  29.7 6.9 %collective-permute-start.6 = (f32[4,3840]{1,0:T(4,128)S(1)}, f32[4,3840]{1,0:T(4,128)S(1)}, u32[]{:S(2)}, u32[]{:S(2)}) collective-permute-start(f32[4,3840]{1,0:T(4,128)S(1)} %add_add_fusion.1), channel_id=1, source_target_pairs={{0,120},{8,112},{16,104},{24,96},{32,88},{40,80},{48,72},{56,64},{... | collective-permute-start | bytes 184328 | tf_op jit(solution)/shard_map/ppermute | solution.py:30
  36.6 5.3 %collective-permute-start.9 = (f32[4,3840]{1,0:T(4,128)S(1)}, f32[4,3840]{1,0:T(4,128)S(1)}, u32[]{:S(2)}, u32[]{:S(2)}) collective-permute-start(f32[4,3840]{1,0:T(4,128)S(1)} %add_add_fusion.refs_2_), channel_id=1, source_target_pairs={{0,4},{4,0},{1,5},{5,1},{2,6},{6,2},{3,7},{7,3},{8,12},{12,8},{9,1... | collective-permute-start | bytes 184328 | tf_op jit(solution)/shard_map/ppermute | solution.py:30
  43.3 4.1 %collective-permute-start.11 = (f32[48,112]{1,0:T(8,128)S(1)}, f32[48,112]{1,0:T(8,128)S(1)}, u32[]{:S(2)}, u32[]{:S(2)}) collective-permute-start(f32[48,112]{1,0:T(8,128)S(1)} %get-tuple-element.31), channel_id=1, source_target_pairs={{0,1},{1,0},{2,3},{3,2},{4,5},{5,4},{6,7},{7,6},{8,9},{9,8},{10,11... | collective-permute-start | bytes 64520 | tf_op jit(solution)/shard_map/ppermute | solution.py:30
  45.3 3.9 %collective-permute-start.12 = (f32[48,112]{1,0:T(8,128)S(1)}, f32[48,112]{1,0:T(8,128)S(1)}, u32[]{:S(2)}, u32[]{:S(2)}) collective-permute-start(f32[48,112]{1,0:T(8,128)S(1)} %get-tuple-element.32), channel_id=1, source_target_pairs={{0,2},{1,3},{2,0},{3,1},{4,6},{5,7},{6,4},{7,5},{8,10},{9,11},{10,... | collective-permute-start | bytes 64520 | tf_op jit(solution)/shard_map/ppermute | solution.py:30
  45.3 4.5 %collective-permute-start.13 = (f32[48,112]{1,0:T(8,128)S(1)}, f32[48,112]{1,0:T(8,128)S(1)}, u32[]{:S(2)}, u32[]{:S(2)}) collective-permute-start(f32[48,112]{1,0:T(8,128)S(1)} %get-tuple-element.33), channel_id=1, source_target_pairs={{0,3},{1,2},{2,1},{3,0},{4,7},{5,6},{6,5},{7,4},{8,11},{9,10},{10,... | collective-permute-start | bytes 64520 | tf_op jit(solution)/shard_map/ppermute | solution.py:30
where the time goes:
time: 50.6 us; the launch traced here: 50.5 us
  starting transfers between devices  26.9 us (53%)
  Pallas kernels  13.1 us (26%)
  waiting for transfers between devices  9.54 us (19%)
  between operations  0.75 us (1%)
    ppermute x14, starting transfers between devices, exchanged(): return lax.ppermute(value, axes, pairs)  26.9 us
    ppermute x14, waiting for transfers between devices, exchanged(): return lax.ppermute(value, axes, pairs)  9.54 us
    pallas_call x2, Pallas kernels, point_table(): pl.pallas_call(functools.partial(points_kernel, flip), out_shape=shape((2...  5.16 us
    pallas_call x1, Pallas kernels, shards(): pl.pallas_call(first_kernel, in_specs=[pl.BlockSpec(memory_space=pltpu.HB...  2.85 us
    pallas_call x2, Pallas kernels, contract(): pl.pallas_call(functools.partial(moments_kernel, flip, comps), out_shape=...  2.61 us
    pallas_call x1, Pallas kernels, shards(): pl.pallas_call(second_kernel, out_shape=table_shapes, compiler_params=PAR...  1.73 us
  transfers between devices with their start and end apart: 14, of which 5 were waited for; matrix products, arithmetic and copies ran while one was open for 0% of the time, Pallas kernels for 16%

commit v1 on v0

--- a/solution.py
+++ b/solution.py
@@ -330,10 +330,11 @@
     far_points = point_table(1)
     near_points = point_table(0)
     for stage in (
-        [dict(y=1, x=1), dict(x=1), dict(y=1)],
-        [dict(y=3, x=3), dict(x=3), dict(y=3)],
+[dict(y=1, x=3), dict(x=3), dict(y=1)],[dict(y=3, x=1), dict(y=3), dict(x=1)],
     ):
-        parts = [exchanged(sums, **flips) for flips in stage]
+        parts = []
+        for flips in stage:
+            parts.append(exchanged(sums, **flips))
         for part in parts:
             sums = sums + part
     other_sums = exchanged(sums, c=1)
@@ -360,7 +361,10 @@
 
     near = contract(0, sums, near_table, near_points, ())
     pieces = contract(1, other_sums, far_table, far_points, (near,))
-    pieces = [pieces[0]] + [exchanged(pieces[turn], g=turn) for turn in (1, 2, 3)]
+    others = []
+    for turn in (1, 2, 3):
+        others.append(exchanged(pieces[turn], g=turn))
+    pieces = [pieces[0]] + others
     grid, moments = pl.pallas_call(
         functools.partial(finish_kernel, comps, few),
         out_shape=[shape((2, own_points), jnp.float32), shape((2, few, comps), jnp.float32)],

time: 50.6 us -> 50.3 us (level)
  waiting for transfers between devices: 9.54 us -> 8.38 us
    ppermute x14, waiting for transfers between devices: 9.54 us -> 8.38 us  [exchanged(): return lax.ppermute(value, axes, pairs)]
where the time goes in v1:
time: 50.3 us; the launch traced here: 49.8 us
  starting transfers between devices  27.3 us (54%)
  Pallas kernels  13.1 us (26%)
  waiting for transfers between devices  8.38 us (17%)
  between operations  0.76 us (2%)
    ppermute x14, starting transfers between devices, exchanged(): return lax.ppermute(value, axes, pairs)  27.3 us
    ppermute x14, waiting for transfers between devices, exchanged(): return lax.ppermute(value, axes, pairs)  8.38 us
    pallas_call x2, Pallas kernels, point_table(): pl.pallas_call(functools.partial(points_kernel, flip), out_shape=shape((2...  5.16 us
    pallas_call x1, Pallas kernels, shards(): pl.pallas_call(first_kernel, in_specs=[pl.BlockSpec(memory_space=pltpu.HB...  2.85 us
    pallas_call x2, Pallas kernels, contract(): pl.pallas_call(functools.partial(moments_kernel, flip, comps), out_shape=...  2.61 us
    pallas_call x1, Pallas kernels, shards(): pl.pallas_call(second_kernel, out_shape=table_shapes, compiler_params=PAR...  1.73 us
  transfers between devices with their start and end apart: 14, of which 5 were waited for; matrix products, arithmetic and copies ran while one was open for 0% of the time, Pallas kernels for 16%

profile of v1, /device:TPU:1, one launch (start us, length us, event | category | flops | bytes accessed | tf_op | source)
XLA Modules:
  0.0 49.8 jit_solution(14186993799929068479)
XLA Ops:
  0.6 2.9 %structure1.1 = (bf16[128,3840]{1,0:T(8,128)(2,1)S(1)}, f32[4,3840]{1,0:T(4,128)S(1)}, f32[8,32]{1,0:T(8,128)S(1)}, s32[3,7680]{1,0:T(4,128)S(1)}, bf16[49,7680]...) custom-call(s32[3,7680]{1,0:T(4,128)} %miller_hbm.1, bf16[49,7680]{1,0:T(8,128)(2,1)} %form_hbm.1, ...), custom_call_target="tpu_custom_call" | custom-call | flops 1761607680 | bytes 1048576 | tf_op jit(solution)/shard_map/structure1/pallas_call | solution.py:275
  3.5 2.5 %collective-permute-start.1 = (f32[8,32]{1,0:T(8,128)S(1)}, f32[8,32]{1,0:T(8,128)S(1)}, u32[]{:S(2)}, u32[]{:S(2)}) collective-permute-start(f32[8,32]{1,0:T(8,128)S(1)} %get-tuple-element.25), channel_id=1, source_target_pairs={{0,1},{1,0},{2,3},{3,2},{4,5},{5,4},{6,7},{7,6},{8,9},{9,8},{10,11... | collective-permute-start | bytes 3080 | tf_op jit(solution)/shard_map/ppermute | solution.py:30
  6.0 1.0 %collective-permute-start = (f32[4,3840]{1,0:T(4,128)S(1)}, f32[4,3840]{1,0:T(4,128)S(1)}, u32[]{:S(2)}, u32[]{:S(2)}) collective-permute-start(f32[4,3840]{1,0:T(4,128)S(1)} %get-tuple-element.24), channel_id=1, source_target_pairs={{0,4},{4,0},{1,5},{5,1},{2,6},{6,2},{3,7},{7,3},{8,12},{12,8},{9,1... | collective-permute-start | bytes 184328 | tf_op jit(solution)/shard_map/ppermute | solution.py:30
  7.0 1.7 %structure0.1 = (bf16[128,3840]{1,0:T(8,128)(2,1)S(1)}, f32[4,3840]{1,0:T(4,128)S(1)}) custom-call(s32[3,7680]{1,0:T(4,128)S(1)} %get-tuple-element.19.miller_ref.refs_0_, bf16[49,7680]{1,0:T(8,128)(2,1)S(1)} %get-tuple-element.20.form_ref.refs_1_, bf16[224,128]{1,0:T(8,128)(2,1)S(1)} %get-tuple-element.21.lhs_ref, f32[8,128]{1,0:T(8,128)S(1)} %get-tuple-element.22.frac_ref), custom_call_target="tpu_custom_call" | custom-call | flops 1761607680 | bytes 1048576 | tf_op jit(solution)/shard_map/structure0/pallas_call | solution.py:308
  8.7 0.0 collective-permute-done.1
  8.7 0.1 pad_maximum_fusion
  8.8 0.0 collective-permute-done
  8.8 3.1 %collective-permute-start.10 = (f32[8,64]{1,0:T(8,128)S(1)}, f32[8,64]{1,0:T(8,128)S(1)}, u32[]{:S(2)}, u32[]{:S(2)}) collective-permute-start(f32[8,64]{1,0:T(8,128)S(1)} %pad_maximum_fusion), channel_id=1, source_target_pairs={{0,2},{1,3},{2,0},{3,1},{4,6},{5,7},{6,4},{7,5},{8,10},{9,11},{10,... | collective-permute-start | bytes 6152 | tf_op jit(solution)/shard_map/ppermute | solution.py:30
  11.9 4.2 %collective-permute-start.2 = (f32[4,3840]{1,0:T(4,128)S(1)}, f32[4,3840]{1,0:T(4,128)S(1)}, u32[]{:S(2)}, u32[]{:S(2)}) collective-permute-start(f32[4,3840]{1,0:T(4,128)S(1)} %add.24), channel_id=1, source_target_pairs={{0,128},{128,0},{1,129},{129,1},{2,130},{130,2},{3,131},{131,3},{4... | collective-permute-start | bytes 184328 | tf_op jit(solution)/shard_map/ppermute | solution.py:30
  16.1 0.0 collective-permute-done.10
  16.1 0.1 pad_maximum_fusion.1.places_ref
  16.2 2.7 %collective-permute-done.2 = f32[4,3840]{1,0:T(4,128)S(1)} collective-permute-done((f32[4,3840]{1,0:T(4,128)S(1)}, f32[4,3840]{1,0:T(4,128)S(1)}, u32[]{:S(2)}, u32[]{:S(2)}) %collective-permute-start.2) | collective-permute-done | bytes 61472 | tf_op jit(solution)/shard_map/ppermute | solution.py:30
  19.0 1.4 %collective-permute-start.5 = (f32[4,3840]{1,0:T(4,128)S(1)}, f32[4,3840]{1,0:T(4,128)S(1)}, u32[]{:S(2)}, u32[]{:S(2)}) collective-permute-start(f32[4,3840]{1,0:T(4,128)S(1)} %add.25), channel_id=1, source_target_pairs={{0,32},{32,0},{64,96},{96,64},{1,33},{33,1},{65,97},{97,65},{2,34}... | collective-permute-start | bytes 184328 | tf_op jit(solution)/shard_map/ppermute | solution.py:30
  20.4 2.5 %collective-permute-start.4 = (f32[4,3840]{1,0:T(4,128)S(1)}, f32[4,3840]{1,0:T(4,128)S(1)}, u32[]{:S(2)}, u32[]{:S(2)}) collective-permute-start(f32[4,3840]{1,0:T(4,128)S(1)} %add.25), channel_id=1, source_target_pairs={{0,24},{8,16},{16,8},{24,0},{1,25},{9,17},{17,9},{25,1},{2,26},{10... | collective-permute-start | bytes 184328 | tf_op jit(solution)/shard_map/ppermute | solution.py:30
  22.8 0.1 collective-permute-start.3
  22.9 2.6 %shard_map.78.refs_4_ = bf16[256,3840]{1,0:T(8,128)(2,1)S(1)} custom-call(s32[3,7680]{1,0:T(4,128)S(1)} %get-tuple-element.19.miller_ref.refs_0_, f32[8,128]{1,0:T(8,128)S(1)} %pad_maximum_fusion.1.places_ref), custom_call_target="tpu_custom_call" | custom-call | flops 1761607680 | bytes 1048576 | tf_op jit(solution)/shard_map/pallas_call | solution.py:319
  25.5 0.0 collective-permute-done.5
  25.5 0.0 collective-permute-done.4
  25.5 2.5 %collective-permute-done.3 = f32[4,3840]{1,0:T(4,128)S(1)} collective-permute-done((f32[4,3840]{1,0:T(4,128)S(1)}, f32[4,3840]{1,0:T(4,128)S(1)}, u32[]{:S(2)}, u32[]{:S(2)}) %collective-permute-start.3) | collective-permute-done | bytes 61472 | tf_op jit(solution)/shard_map/ppermute | solution.py:30
  28.1 0.1 collective-permute-start.8
  28.2 2.1 %collective-permute-start.7 = (f32[4,3840]{1,0:T(4,128)S(1)}, f32[4,3840]{1,0:T(4,128)S(1)}, u32[]{:S(2)}, u32[]{:S(2)}) collective-permute-start(f32[4,3840]{1,0:T(4,128)S(1)} %add_add_fusion.1), channel_id=1, source_target_pairs={{0,96},{32,64},{64,32},{96,0},{1,97},{33,65},{65,33},{97,1},{2,98}... | collective-permute-start | bytes 184328 | tf_op jit(solution)/shard_map/ppermute | solution.py:30
  30.3 1.7 %collective-permute-start.6 = (f32[4,3840]{1,0:T(4,128)S(1)}, f32[4,3840]{1,0:T(4,128)S(1)}, u32[]{:S(2)}, u32[]{:S(2)}) collective-permute-start(f32[4,3840]{1,0:T(4,128)S(1)} %add_add_fusion.1), channel_id=1, source_target_pairs={{0,104},{8,96},{16,120},{24,112},{32,72},{40,64},{48,88},{56,80},{... | collective-permute-start | bytes 184328 | tf_op jit(solution)/shard_map/ppermute | solution.py:30
  32.0 2.6 %shard_map.77.refs_4_ = bf16[256,3840]{1,0:T(8,128)(2,1)S(1)} custom-call(s32[3,7680]{1,0:T(4,128)S(1)} %get-tuple-element.19.miller_ref.refs_0_, f32[8,128]{1,0:T(8,128)S(1)} %pad_maximum_fusion.1.places_ref), custom_call_target="tpu_custom_call" | custom-call | flops 1761607680 | bytes 1048576 | tf_op jit(solution)/shard_map/pallas_call | solution.py:319
  34.6 0.0 collective-permute-done.8
  34.6 0.0 collective-permute-done.7
  34.6 0.8 %collective-permute-done.6 = f32[4,3840]{1,0:T(4,128)S(1)} collective-permute-done((f32[4,3840]{1,0:T(4,128)S(1)}, f32[4,3840]{1,0:T(4,128)S(1)}, u32[]{:S(2)}, u32[]{:S(2)}) %collective-permute-start.6) | collective-permute-done | bytes 61472 | tf_op jit(solution)/shard_map/ppermute | solution.py:30
  35.5 4.5 %collective-permute-start.9 = (f32[4,3840]{1,0:T(4,128)S(1)}, f32[4,3840]{1,0:T(4,128)S(1)}, u32[]{:S(2)}, u32[]{:S(2)}) collective-permute-start(f32[4,3840]{1,0:T(4,128)S(1)} %add_add_fusion.refs_2_), channel_id=1, source_target_pairs={{0,4},{4,0},{1,5},{5,1},{2,6},{6,2},{3,7},{7,3},{8,12},{12,8},{9,1... | collective-permute-start | bytes 184328 | tf_op jit(solution)/shard_map/ppermute | solution.py:30
  40.0 1.2 %shard_map.79.refs_5_ = f32[112,192]{1,0:T(8,128)S(1)} custom-call(s32[3,7680]{1,0:T(4,128)S(1)} %get-tuple-element.19.miller_ref.refs_0_, bf16[49,7680]{1,0:T(8,128)(2,1)S(1)} %get-tuple-element.20.form_ref.refs_1_, f32[4,3840]{1,0:T(4,128)S(1)} %add_add_fusion.refs_2_, bf16[128,3840]{1,0:T(8,128)(2,1)S(1)} %get-tuple-element.29.refs_3_, ...), custom_call_target="tpu_custom_call" | custom-call | flops 1761607680 | bytes 1048576 | tf_op jit(solution)/shard_map/pallas_call | solution.py:349
  41.2 0.0 collective-permute-done.9.refs_2_
  41.2 1.4 %shard_map.80 = (f32[48,112]{1,0:T(8,128)S(1)}, f32[48,112]{1,0:T(8,128)S(1)}, f32[48,112]{1,0:T(8,128)S(1)}, f32[48,112]{1,0:T(8,128)S(1)}) custom-call(s32[3,7680]{1,0:T(4,128)S(1)} %get-tuple-element.19.miller_ref.refs_0_, bf16[49,7680]{1,0:T(8,128)(2,1)S(1)} %get-tuple-element.20.form_ref.refs_1_, f32[4,3840]{1,0:T(4,128)S(1)} %collective-permute-done.9.refs_2_, ...), custom_call_target="tpu_custom_call" | custom-call | flops 1761607680 | bytes 1048576 | tf_op jit(solution)/shard_map/pallas_call | solution.py:349
  42.6 2.0 %collective-permute-start.11 = (f32[48,112]{1,0:T(8,128)S(1)}, f32[48,112]{1,0:T(8,128)S(1)}, u32[]{:S(2)}, u32[]{:S(2)}) collective-permute-start(f32[48,112]{1,0:T(8,128)S(1)} %get-tuple-element.31), channel_id=1, source_target_pairs={{0,1},{1,0},{2,3},{3,2},{4,5},{5,4},{6,7},{7,6},{8,9},{9,8},{10,11... | collective-permute-start | bytes 64520 | tf_op jit(solution)/shard_map/ppermute | solution.py:30
  44.6 0.0 collective-permute-start.12
  44.6 2.2 %collective-permute-start.13 = (f32[48,112]{1,0:T(8,128)S(1)}, f32[48,112]{1,0:T(8,128)S(1)}, u32[]{:S(2)}, u32[]{:S(2)}) collective-permute-start(f32[48,112]{1,0:T(8,128)S(1)} %get-tuple-element.33), channel_id=1, source_target_pairs={{0,3},{1,2},{2,1},{3,0},{4,7},{5,6},{6,5},{7,4},{8,11},{9,10},{10,... | collective-permute-start | bytes 64520 | tf_op jit(solution)/shard_map/ppermute | solution.py:30
  46.7 0.0 collective-permute-done.11.second_ref
  46.7 1.7 %collective-permute-done.12.third_ref = f32[48,112]{1,0:T(8,128)S(1)} collective-permute-done((f32[48,112]{1,0:T(8,128)S(1)}, f32[48,112]{1,0:T(8,128)S(1)}, u32[]{:S(2)}, u32[]{:S(2)}) %collective-permute-start.12) | collective-permute-done | bytes 21536 | tf_op jit(solution)/shard_map/ppermute | solution.py:30
  48.5 0.6 %collective-permute-done.13.fourth_ref = f32[48,112]{1,0:T(8,128)S(1)} collective-permute-done((f32[48,112]{1,0:T(8,128)S(1)}, f32[48,112]{1,0:T(8,128)S(1)}, u32[]{:S(2)}, u32[]{:S(2)}) %collective-permute-start.13) | collective-permute-done | bytes 21536 | tf_op jit(solution)/shard_map/ppermute | solution.py:30
  49.0 0.8 %finish.1 = (f32[2,32]{1,0:T(2,128)}, f32[2,16,49]{2,1,0:T(8,128)}) custom-call(f32[48,112]{1,0:T(8,128)S(1)} %get-tuple-element.30.first_ref, f32[48,112]{1,0:T(8,128)S(1)} %collective-permute-done.11.second_ref, f32[48,112]{1,0:T(8,128)S(1)} %collective-permute-done.12.third_ref, f32[48,112]{1,0:T(8,128)S(1)} %collective-permute-done.13.fourth_ref), custom_call_target="tpu_custom_call" | custom-call | flops 1048576 | bytes 1048576 | tf_op jit(solution)/shard_map/finish/pallas_call | solution.py:368
  (4 shorter events, 0.1 us)
Async XLA Ops:
  3.5 5.2 %collective-permute-start.1 = (f32[8,32]{1,0:T(8,128)S(1)}, f32[8,32]{1,0:T(8,128)S(1)}, u32[]{:S(2)}, u32[]{:S(2)}) collective-permute-start(f32[8,32]{1,0:T(8,128)S(1)} %get-tuple-element.25), channel_id=1, source_target_pairs={{0,1},{1,0},{2,3},{3,2},{4,5},{5,4},{6,7},{7,6},{8,9},{9,8},{10,11... | collective-permute-start | bytes 3080 | tf_op jit(solution)/shard_map/ppermute | solution.py:30
  6.0 2.8 %collective-permute-start = (f32[4,3840]{1,0:T(4,128)S(1)}, f32[4,3840]{1,0:T(4,128)S(1)}, u32[]{:S(2)}, u32[]{:S(2)}) collective-permute-start(f32[4,3840]{1,0:T(4,128)S(1)} %get-tuple-element.24), channel_id=1, source_target_pairs={{0,4},{4,0},{1,5},{5,1},{2,6},{6,2},{3,7},{7,3},{8,12},{12,8},{9,1... | collective-permute-start | bytes 184328 | tf_op jit(solution)/shard_map/ppermute | solution.py:30
  8.8 7.3 %collective-permute-start.10 = (f32[8,64]{1,0:T(8,128)S(1)}, f32[8,64]{1,0:T(8,128)S(1)}, u32[]{:S(2)}, u32[]{:S(2)}) collective-permute-start(f32[8,64]{1,0:T(8,128)S(1)} %pad_maximum_fusion), channel_id=1, source_target_pairs={{0,2},{1,3},{2,0},{3,1},{4,6},{5,7},{6,4},{7,5},{8,10},{9,11},{10,... | collective-permute-start | bytes 6152 | tf_op jit(solution)/shard_map/ppermute | solution.py:30
  11.9 7.0 %collective-permute-start.2 = (f32[4,3840]{1,0:T(4,128)S(1)}, f32[4,3840]{1,0:T(4,128)S(1)}, u32[]{:S(2)}, u32[]{:S(2)}) collective-permute-start(f32[4,3840]{1,0:T(4,128)S(1)} %add.24), channel_id=1, source_target_pairs={{0,128},{128,0},{1,129},{129,1},{2,130},{130,2},{3,131},{131,3},{4... | collective-permute-start | bytes 184328 | tf_op jit(solution)/shard_map/ppermute | solution.py:30
  19.0 6.5 %collective-permute-start.5 = (f32[4,3840]{1,0:T(4,128)S(1)}, f32[4,3840]{1,0:T(4,128)S(1)}, u32[]{:S(2)}, u32[]{:S(2)}) collective-permute-start(f32[4,3840]{1,0:T(4,128)S(1)} %add.25), channel_id=1, source_target_pairs={{0,32},{32,0},{64,96},{96,64},{1,33},{33,1},{65,97},{97,65},{2,34}... | collective-permute-start | bytes 184328 | tf_op jit(solution)/shard_map/ppermute | solution.py:30
  20.4 5.2 %collective-permute-start.4 = (f32[4,3840]{1,0:T(4,128)S(1)}, f32[4,3840]{1,0:T(4,128)S(1)}, u32[]{:S(2)}, u32[]{:S(2)}) collective-permute-start(f32[4,3840]{1,0:T(4,128)S(1)} %add.25), channel_id=1, source_target_pairs={{0,24},{8,16},{16,8},{24,0},{1,25},{9,17},{17,9},{25,1},{2,26},{10... | collective-permute-start | bytes 184328 | tf_op jit(solution)/shard_map/ppermute | solution.py:30
  22.8 5.2 %collective-permute-start.3 = (f32[4,3840]{1,0:T(4,128)S(1)}, f32[4,3840]{1,0:T(4,128)S(1)}, u32[]{:S(2)}, u32[]{:S(2)}) collective-permute-start(f32[4,3840]{1,0:T(4,128)S(1)} %add.25), channel_id=1, source_target_pairs={{0,56},{8,48},{16,40},{24,32},{32,24},{40,16},{48,8},{56,0},{64,12... | collective-permute-start | bytes 184328 | tf_op jit(solution)/shard_map/ppermute | solution.py:30
  28.1 6.5 %collective-permute-start.8 = (f32[4,3840]{1,0:T(4,128)S(1)}, f32[4,3840]{1,0:T(4,128)S(1)}, u32[]{:S(2)}, u32[]{:S(2)}) collective-permute-start(f32[4,3840]{1,0:T(4,128)S(1)} %add_add_fusion.1), channel_id=1, source_target_pairs={{0,8},{8,0},{16,24},{24,16},{1,9},{9,1},{17,25},{25,17},{2,10},{10... | collective-permute-start | bytes 184328 | tf_op jit(solution)/shard_map/ppermute | solution.py:30
  28.2 6.4 %collective-permute-start.7 = (f32[4,3840]{1,0:T(4,128)S(1)}, f32[4,3840]{1,0:T(4,128)S(1)}, u32[]{:S(2)}, u32[]{:S(2)}) collective-permute-start(f32[4,3840]{1,0:T(4,128)S(1)} %add_add_fusion.1), channel_id=1, source_target_pairs={{0,96},{32,64},{64,32},{96,0},{1,97},{33,65},{65,33},{97,1},{2,98}... | collective-permute-start | bytes 184328 | tf_op jit(solution)/shard_map/ppermute | solution.py:30
  30.3 5.2 %collective-permute-start.6 = (f32[4,3840]{1,0:T(4,128)S(1)}, f32[4,3840]{1,0:T(4,128)S(1)}, u32[]{:S(2)}, u32[]{:S(2)}) collective-permute-start(f32[4,3840]{1,0:T(4,128)S(1)} %add_add_fusion.1), channel_id=1, source_target_pairs={{0,104},{8,96},{16,120},{24,112},{32,72},{40,64},{48,88},{56,80},{... | collective-permute-start | bytes 184328 | tf_op jit(solution)/shard_map/ppermute | solution.py:30
  35.5 5.7 %collective-permute-start.9 = (f32[4,3840]{1,0:T(4,128)S(1)}, f32[4,3840]{1,0:T(4,128)S(1)}, u32[]{:S(2)}, u32[]{:S(2)}) collective-permute-start(f32[4,3840]{1,0:T(4,128)S(1)} %add_add_fusion.refs_2_), channel_id=1, source_target_pairs={{0,4},{4,0},{1,5},{5,1},{2,6},{6,2},{3,7},{7,3},{8,12},{12,8},{9,1... | collective-permute-start | bytes 184328 | tf_op jit(solution)/shard_map/ppermute | solution.py:30
  42.6 4.1 %collective-permute-start.11 = (f32[48,112]{1,0:T(8,128)S(1)}, f32[48,112]{1,0:T(8,128)S(1)}, u32[]{:S(2)}, u32[]{:S(2)}) collective-permute-start(f32[48,112]{1,0:T(8,128)S(1)} %get-tuple-element.31), channel_id=1, source_target_pairs={{0,1},{1,0},{2,3},{3,2},{4,5},{5,4},{6,7},{7,6},{8,9},{9,8},{10,11... | collective-permute-start | bytes 64520 | tf_op jit(solution)/shard_map/ppermute | solution.py:30
  44.6 3.9 %collective-permute-start.12 = (f32[48,112]{1,0:T(8,128)S(1)}, f32[48,112]{1,0:T(8,128)S(1)}, u32[]{:S(2)}, u32[]{:S(2)}) collective-permute-start(f32[48,112]{1,0:T(8,128)S(1)} %get-tuple-element.32), channel_id=1, source_target_pairs={{0,2},{1,3},{2,0},{3,1},{4,6},{5,7},{6,4},{7,5},{8,10},{9,11},{10,... | collective-permute-start | bytes 64520 | tf_op jit(solution)/shard_map/ppermute | solution.py:30
  44.6 4.5 %collective-permute-start.13 = (f32[48,112]{1,0:T(8,128)S(1)}, f32[48,112]{1,0:T(8,128)S(1)}, u32[]{:S(2)}, u32[]{:S(2)}) collective-permute-start(f32[48,112]{1,0:T(8,128)S(1)} %get-tuple-element.33), channel_id=1, source_target_pairs={{0,3},{1,2},{2,1},{3,0},{4,7},{5,6},{6,5},{7,4},{8,11},{9,10},{10,... | collective-permute-start | bytes 64520 | tf_op jit(solution)/shard_map/ppermute | solution.py:30

commit v2 on v1

--- a/solution.py
+++ b/solution.py
@@ -139,8 +139,6 @@
         lhs_scr[low + ROWS : low + ROWS + comps, :] = jnp.concatenate([poles * odd, -(poles * even)], axis=1)
     lhs = lhs_scr[...].astype(jnp.bfloat16)
     lhs_ref[...] = lhs
-    copies[2].wait()
-    structure_into(base, columns, lhs, miller_ref, form_ref, table_ref, sums_ref, copies[3].wait)
     copies[4].wait()
     copies[5].wait()
     points = owner_ref.shape[1]
@@ -148,6 +146,8 @@
     for axis in range(3):
         spread = jnp.where(chosen, columns[axis], 0.0)
         places_ref[axis : axis + 1, :] = jnp.sum(spread, axis=0, keepdims=True) + offsets_ref[axis : axis + 1, :]
+    copies[2].wait()
+    structure_into(base, columns, lhs, miller_ref, form_ref, table_ref, sums_ref, copies[3].wait)
     copies[6].wait()
 
 
@@ -193,7 +193,7 @@
     points = points_ref.shape[0] // 2
     contract = (((1,), (1,)), ((), ()))
     total = before_ref[...] if flip else None
-    chunk = width // 3
+    chunk = width // 15
     for slot in range(form_scr.shape[0]):
         form_scr[slot, comps:ROWS, :] = ones
     for first in range(0, width, chunk):
@@ -240,7 +240,7 @@
 
 def finish_kernel(comps, atoms, first_ref, second_ref, third_ref, fourth_ref, grid_ref, moments_ref):
     total = (first_ref[...] + second_ref[...]) + (third_ref[...] + fourth_ref[...])
-    turned = total.T
+    turned = total[atoms:].T
     place = lax.broadcasted_iota(jnp.int32, (atoms, comps), 1)
     sign = jnp.zeros((atoms, comps), jnp.float32)
     degree = 0
@@ -251,7 +251,7 @@
     for density in range(2):
         low = ROWS * density
         moments_ref[density] = total[0:atoms, low : low + comps] * sign
-        grid_ref[density : density + 1, :] = turned[low + comps : low + comps + 1, atoms:]
+        grid_ref[density : density + 1, :] = turned[low + comps : low + comps + 1, :]
 
 
 def cost(flops):
@@ -304,7 +304,8 @@
     )
 
     arrived = exchanged(far_sums, c=1)
-    places = jnp.concatenate([places, exchanged(places, g=1)], axis=1)
+    others = exchanged(places, g=1)
+    places = jnp.concatenate([places, others], axis=1)
     near_table, near_sums = pl.pallas_call(
         second_kernel,
         out_shape=table_shapes,
@@ -329,9 +330,11 @@
     sums = sums + crossed
     far_points = point_table(1)
     near_points = point_table(0)
-    for stage in (
-[dict(y=1, x=3), dict(x=3), dict(y=1)],[dict(y=3, x=1), dict(y=3), dict(x=1)],
-    ):
+    stages = (
+        (dict(y=1, x=3), dict(x=3), dict(y=1)),
+        (dict(y=3, x=1), dict(y=3), dict(x=1)),
+    )
+    for stage in stages:
         parts = []
         for flips in stage:
             parts.append(exchanged(sums, **flips))

time: 50.3 us -> 50 us (level)
  no operation moved by 1% of the time
where the time goes in v2:
time: 50 us; the launch traced here: 49.4 us
  starting transfers between devices  27.3 us (55%)
  Pallas kernels  12.7 us (25%)
  waiting for transfers between devices  8.38 us (17%)
  between operations  0.76 us (2%)
    ppermute x14, starting transfers between devices, exchanged(): return lax.ppermute(value, axes, pairs)  27.3 us
    ppermute x14, waiting for transfers between devices, exchanged(): return lax.ppermute(value, axes, pairs)  8.38 us
    pallas_call x2, Pallas kernels, point_table(): pl.pallas_call(functools.partial(points_kernel, flip), out_shape=shape((2...  5.16 us
    pallas_call x1, Pallas kernels, shards(): pl.pallas_call(first_kernel, in_specs=[pl.BlockSpec(memory_space=pltpu.HB...  2.85 us
    pallas_call x2, Pallas kernels, contract(): pl.pallas_call(functools.partial(moments_kernel, flip, comps), out_shape=...  2.25 us
    pallas_call x1, Pallas kernels, shards(): pl.pallas_call(second_kernel, out_shape=table_shapes, compiler_params=PAR...  1.72 us
  transfers between devices with their start and end apart: 14, of which 5 were waited for; matrix products, arithmetic and copies ran while one was open for 0% of the time, Pallas kernels for 16%

profile of v2, /device:TPU:1, one launch (start us, length us, event | category | flops | bytes accessed | tf_op | source)
XLA Modules:
  0.0 49.4 jit_solution(355653147880232854)
XLA Ops:
  0.6 2.9 %structure1.1 = (bf16[128,3840]{1,0:T(8,128)(2,1)S(1)}, f32[4,3840]{1,0:T(4,128)S(1)}, f32[8,32]{1,0:T(8,128)S(1)}, s32[3,7680]{1,0:T(4,128)S(1)}, bf16[49,7680]...) custom-call(s32[3,7680]{1,0:T(4,128)} %miller_hbm.1, bf16[49,7680]{1,0:T(8,128)(2,1)} %form_hbm.1, ...), custom_call_target="tpu_custom_call" | custom-call | flops 1761607680 | bytes 1048576 | tf_op jit(solution)/shard_map/structure1/pallas_call | solution.py:275
  3.5 2.5 %collective-permute-start.1 = (f32[8,32]{1,0:T(8,128)S(1)}, f32[8,32]{1,0:T(8,128)S(1)}, u32[]{:S(2)}, u32[]{:S(2)}) collective-permute-start(f32[8,32]{1,0:T(8,128)S(1)} %get-tuple-element.25), channel_id=1, source_target_pairs={{0,1},{1,0},{2,3},{3,2},{4,5},{5,4},{6,7},{7,6},{8,9},{9,8},{10,11... | collective-permute-start | bytes 3080 | tf_op jit(solution)/shard_map/ppermute | solution.py:30
  6.0 1.0 %collective-permute-start = (f32[4,3840]{1,0:T(4,128)S(1)}, f32[4,3840]{1,0:T(4,128)S(1)}, u32[]{:S(2)}, u32[]{:S(2)}) collective-permute-start(f32[4,3840]{1,0:T(4,128)S(1)} %get-tuple-element.24), channel_id=1, source_target_pairs={{0,4},{4,0},{1,5},{5,1},{2,6},{6,2},{3,7},{7,3},{8,12},{12,8},{9,1... | collective-permute-start | bytes 184328 | tf_op jit(solution)/shard_map/ppermute | solution.py:30
  7.0 1.7 %structure0.1 = (bf16[128,3840]{1,0:T(8,128)(2,1)S(1)}, f32[4,3840]{1,0:T(4,128)S(1)}) custom-call(s32[3,7680]{1,0:T(4,128)S(1)} %get-tuple-element.19.miller_ref.refs_0_, bf16[49,7680]{1,0:T(8,128)(2,1)S(1)} %get-tuple-element.20.form_ref.refs_1_, bf16[224,128]{1,0:T(8,128)(2,1)S(1)} %get-tuple-element.21.lhs_ref, f32[8,128]{1,0:T(8,128)S(1)} %get-tuple-element.22.frac_ref), custom_call_target="tpu_custom_call" | custom-call | flops 1761607680 | bytes 1048576 | tf_op jit(solution)/shard_map/structure0/pallas_call | solution.py:309
  8.7 0.0 collective-permute-done.1
  8.7 0.1 pad_maximum_fusion
  8.8 0.0 collective-permute-done
  8.8 3.1 %collective-permute-start.10 = (f32[8,64]{1,0:T(8,128)S(1)}, f32[8,64]{1,0:T(8,128)S(1)}, u32[]{:S(2)}, u32[]{:S(2)}) collective-permute-start(f32[8,64]{1,0:T(8,128)S(1)} %pad_maximum_fusion), channel_id=1, source_target_pairs={{0,2},{1,3},{2,0},{3,1},{4,6},{5,7},{6,4},{7,5},{8,10},{9,11},{10,... | collective-permute-start | bytes 6152 | tf_op jit(solution)/shard_map/ppermute | solution.py:30
  11.9 4.2 %collective-permute-start.2 = (f32[4,3840]{1,0:T(4,128)S(1)}, f32[4,3840]{1,0:T(4,128)S(1)}, u32[]{:S(2)}, u32[]{:S(2)}) collective-permute-start(f32[4,3840]{1,0:T(4,128)S(1)} %add.24), channel_id=1, source_target_pairs={{0,128},{128,0},{1,129},{129,1},{2,130},{130,2},{3,131},{131,3},{4... | collective-permute-start | bytes 184328 | tf_op jit(solution)/shard_map/ppermute | solution.py:30
  16.1 0.0 collective-permute-done.10
  16.1 0.1 pad_maximum_fusion.1.places_ref
  16.2 2.7 %collective-permute-done.2 = f32[4,3840]{1,0:T(4,128)S(1)} collective-permute-done((f32[4,3840]{1,0:T(4,128)S(1)}, f32[4,3840]{1,0:T(4,128)S(1)}, u32[]{:S(2)}, u32[]{:S(2)}) %collective-permute-start.2) | collective-permute-done | bytes 61472 | tf_op jit(solution)/shard_map/ppermute | solution.py:30
  19.0 1.4 %collective-permute-start.5 = (f32[4,3840]{1,0:T(4,128)S(1)}, f32[4,3840]{1,0:T(4,128)S(1)}, u32[]{:S(2)}, u32[]{:S(2)}) collective-permute-start(f32[4,3840]{1,0:T(4,128)S(1)} %add.25), channel_id=1, source_target_pairs={{0,32},{32,0},{64,96},{96,64},{1,33},{33,1},{65,97},{97,65},{2,34}... | collective-permute-start | bytes 184328 | tf_op jit(solution)/shard_map/ppermute | solution.py:30
  20.3 2.5 %collective-permute-start.4 = (f32[4,3840]{1,0:T(4,128)S(1)}, f32[4,3840]{1,0:T(4,128)S(1)}, u32[]{:S(2)}, u32[]{:S(2)}) collective-permute-start(f32[4,3840]{1,0:T(4,128)S(1)} %add.25), channel_id=1, source_target_pairs={{0,24},{8,16},{16,8},{24,0},{1,25},{9,17},{17,9},{25,1},{2,26},{10... | collective-permute-start | bytes 184328 | tf_op jit(solution)/shard_map/ppermute | solution.py:30
  22.8 0.1 collective-permute-start.3
  22.9 2.6 %shard_map.78.refs_4_ = bf16[256,3840]{1,0:T(8,128)(2,1)S(1)} custom-call(s32[3,7680]{1,0:T(4,128)S(1)} %get-tuple-element.19.miller_ref.refs_0_, f32[8,128]{1,0:T(8,128)S(1)} %pad_maximum_fusion.1.places_ref), custom_call_target="tpu_custom_call" | custom-call | flops 1761607680 | bytes 1048576 | tf_op jit(solution)/shard_map/pallas_call | solution.py:320
  25.5 0.0 collective-permute-done.5
  25.5 0.0 collective-permute-done.4
  25.5 2.5 %collective-permute-done.3 = f32[4,3840]{1,0:T(4,128)S(1)} collective-permute-done((f32[4,3840]{1,0:T(4,128)S(1)}, f32[4,3840]{1,0:T(4,128)S(1)}, u32[]{:S(2)}, u32[]{:S(2)}) %collective-permute-start.3) | collective-permute-done | bytes 61472 | tf_op jit(solution)/shard_map/ppermute | solution.py:30
  28.0 0.1 collective-permute-start.8
  28.1 2.1 %collective-permute-start.7 = (f32[4,3840]{1,0:T(4,128)S(1)}, f32[4,3840]{1,0:T(4,128)S(1)}, u32[]{:S(2)}, u32[]{:S(2)}) collective-permute-start(f32[4,3840]{1,0:T(4,128)S(1)} %add_add_fusion.1), channel_id=1, source_target_pairs={{0,96},{32,64},{64,32},{96,0},{1,97},{33,65},{65,33},{97,1},{2,98}... | collective-permute-start | bytes 184328 | tf_op jit(solution)/shard_map/ppermute | solution.py:30
  30.2 1.7 %collective-permute-start.6 = (f32[4,3840]{1,0:T(4,128)S(1)}, f32[4,3840]{1,0:T(4,128)S(1)}, u32[]{:S(2)}, u32[]{:S(2)}) collective-permute-start(f32[4,3840]{1,0:T(4,128)S(1)} %add_add_fusion.1), channel_id=1, source_target_pairs={{0,104},{8,96},{16,120},{24,112},{32,72},{40,64},{48,88},{56,80},{... | collective-permute-start | bytes 184328 | tf_op jit(solution)/shard_map/ppermute | solution.py:30
  32.0 2.6 %shard_map.77.refs_4_ = bf16[256,3840]{1,0:T(8,128)(2,1)S(1)} custom-call(s32[3,7680]{1,0:T(4,128)S(1)} %get-tuple-element.19.miller_ref.refs_0_, f32[8,128]{1,0:T(8,128)S(1)} %pad_maximum_fusion.1.places_ref), custom_call_target="tpu_custom_call" | custom-call | flops 1761607680 | bytes 1048576 | tf_op jit(solution)/shard_map/pallas_call | solution.py:320
  34.6 0.0 collective-permute-done.8
  34.6 0.0 collective-permute-done.7
  34.6 0.8 %collective-permute-done.6 = f32[4,3840]{1,0:T(4,128)S(1)} collective-permute-done((f32[4,3840]{1,0:T(4,128)S(1)}, f32[4,3840]{1,0:T(4,128)S(1)}, u32[]{:S(2)}, u32[]{:S(2)}) %collective-permute-start.6) | collective-permute-done | bytes 61472 | tf_op jit(solution)/shard_map/ppermute | solution.py:30
  35.5 4.5 %collective-permute-start.9 = (f32[4,3840]{1,0:T(4,128)S(1)}, f32[4,3840]{1,0:T(4,128)S(1)}, u32[]{:S(2)}, u32[]{:S(2)}) collective-permute-start(f32[4,3840]{1,0:T(4,128)S(1)} %add_add_fusion.refs_2_), channel_id=1, source_target_pairs={{0,4},{4,0},{1,5},{5,1},{2,6},{6,2},{3,7},{7,3},{8,12},{12,8},{9,1... | collective-permute-start | bytes 184328 | tf_op jit(solution)/shard_map/ppermute | solution.py:30
  40.0 1.1 %shard_map.79.refs_5_ = f32[112,192]{1,0:T(8,128)S(1)} custom-call(s32[3,7680]{1,0:T(4,128)S(1)} %get-tuple-element.19.miller_ref.refs_0_, bf16[49,7680]{1,0:T(8,128)(2,1)S(1)} %get-tuple-element.20.form_ref.refs_1_, f32[4,3840]{1,0:T(4,128)S(1)} %add_add_fusion.refs_2_, bf16[128,3840]{1,0:T(8,128)(2,1)S(1)} %get-tuple-element.29.refs_3_, ...), custom_call_target="tpu_custom_call" | custom-call | flops 1761607680 | bytes 1048576 | tf_op jit(solution)/shard_map/pallas_call | solution.py:352
  41.1 0.0 collective-permute-done.9.refs_2_
  41.1 1.2 %shard_map.80 = (f32[48,112]{1,0:T(8,128)S(1)}, f32[48,112]{1,0:T(8,128)S(1)}, f32[48,112]{1,0:T(8,128)S(1)}, f32[48,112]{1,0:T(8,128)S(1)}) custom-call(s32[3,7680]{1,0:T(4,128)S(1)} %get-tuple-element.19.miller_ref.refs_0_, bf16[49,7680]{1,0:T(8,128)(2,1)S(1)} %get-tuple-element.20.form_ref.refs_1_, f32[4,3840]{1,0:T(4,128)S(1)} %collective-permute-done.9.refs_2_, ...), custom_call_target="tpu_custom_call" | custom-call | flops 1761607680 | bytes 1048576 | tf_op jit(solution)/shard_map/pallas_call | solution.py:352
  42.2 2.0 %collective-permute-start.11 = (f32[48,112]{1,0:T(8,128)S(1)}, f32[48,112]{1,0:T(8,128)S(1)}, u32[]{:S(2)}, u32[]{:S(2)}) collective-permute-start(f32[48,112]{1,0:T(8,128)S(1)} %get-tuple-element.31), channel_id=1, source_target_pairs={{0,1},{1,0},{2,3},{3,2},{4,5},{5,4},{6,7},{7,6},{8,9},{9,8},{10,11... | collective-permute-start | bytes 64520 | tf_op jit(solution)/shard_map/ppermute | solution.py:30
  44.2 0.0 collective-permute-start.12
  44.2 2.2 %collective-permute-start.13 = (f32[48,112]{1,0:T(8,128)S(1)}, f32[48,112]{1,0:T(8,128)S(1)}, u32[]{:S(2)}, u32[]{:S(2)}) collective-permute-start(f32[48,112]{1,0:T(8,128)S(1)} %get-tuple-element.33), channel_id=1, source_target_pairs={{0,3},{1,2},{2,1},{3,0},{4,7},{5,6},{6,5},{7,4},{8,11},{9,10},{10,... | collective-permute-start | bytes 64520 | tf_op jit(solution)/shard_map/ppermute | solution.py:30
  46.4 0.0 collective-permute-done.11.second_ref
  46.4 1.5 %collective-permute-done.12.third_ref = f32[48,112]{1,0:T(8,128)S(1)} collective-permute-done((f32[48,112]{1,0:T(8,128)S(1)}, f32[48,112]{1,0:T(8,128)S(1)}, u32[]{:S(2)}, u32[]{:S(2)}) %collective-permute-start.12) | collective-permute-done | bytes 21536 | tf_op jit(solution)/shard_map/ppermute | solution.py:30
  47.9 0.8 %collective-permute-done.13.fourth_ref = f32[48,112]{1,0:T(8,128)S(1)} collective-permute-done((f32[48,112]{1,0:T(8,128)S(1)}, f32[48,112]{1,0:T(8,128)S(1)}, u32[]{:S(2)}, u32[]{:S(2)}) %collective-permute-start.13) | collective-permute-done | bytes 21536 | tf_op jit(solution)/shard_map/ppermute | solution.py:30
  48.7 0.8 %finish.1 = (f32[2,32]{1,0:T(2,128)}, f32[2,16,49]{2,1,0:T(8,128)}) custom-call(f32[48,112]{1,0:T(8,128)S(1)} %get-tuple-element.30.first_ref, f32[48,112]{1,0:T(8,128)S(1)} %collective-permute-done.11.second_ref, f32[48,112]{1,0:T(8,128)S(1)} %collective-permute-done.12.third_ref, f32[48,112]{1,0:T(8,128)S(1)} %collective-permute-done.13.fourth_ref), custom_call_target="tpu_custom_call" | custom-call | flops 1048576 | bytes 1048576 | tf_op jit(solution)/shard_map/finish/pallas_call | solution.py:371
  (4 shorter events, 0.1 us)
Async XLA Ops:
  3.5 5.2 %collective-permute-start.1 = (f32[8,32]{1,0:T(8,128)S(1)}, f32[8,32]{1,0:T(8,128)S(1)}, u32[]{:S(2)}, u32[]{:S(2)}) collective-permute-start(f32[8,32]{1,0:T(8,128)S(1)} %get-tuple-element.25), channel_id=1, source_target_pairs={{0,1},{1,0},{2,3},{3,2},{4,5},{5,4},{6,7},{7,6},{8,9},{9,8},{10,11... | collective-permute-start | bytes 3080 | tf_op jit(solution)/shard_map/ppermute | solution.py:30
  6.0 2.8 %collective-permute-start = (f32[4,3840]{1,0:T(4,128)S(1)}, f32[4,3840]{1,0:T(4,128)S(1)}, u32[]{:S(2)}, u32[]{:S(2)}) collective-permute-start(f32[4,3840]{1,0:T(4,128)S(1)} %get-tuple-element.24), channel_id=1, source_target_pairs={{0,4},{4,0},{1,5},{5,1},{2,6},{6,2},{3,7},{7,3},{8,12},{12,8},{9,1... | collective-permute-start | bytes 184328 | tf_op jit(solution)/shard_map/ppermute | solution.py:30
  8.8 7.3 %collective-permute-start.10 = (f32[8,64]{1,0:T(8,128)S(1)}, f32[8,64]{1,0:T(8,128)S(1)}, u32[]{:S(2)}, u32[]{:S(2)}) collective-permute-start(f32[8,64]{1,0:T(8,128)S(1)} %pad_maximum_fusion), channel_id=1, source_target_pairs={{0,2},{1,3},{2,0},{3,1},{4,6},{5,7},{6,4},{7,5},{8,10},{9,11},{10,... | collective-permute-start | bytes 6152 | tf_op jit(solution)/shard_map/ppermute | solution.py:30
  11.9 7.0 %collective-permute-start.2 = (f32[4,3840]{1,0:T(4,128)S(1)}, f32[4,3840]{1,0:T(4,128)S(1)}, u32[]{:S(2)}, u32[]{:S(2)}) collective-permute-start(f32[4,3840]{1,0:T(4,128)S(1)} %add.24), channel_id=1, source_target_pairs={{0,128},{128,0},{1,129},{129,1},{2,130},{130,2},{3,131},{131,3},{4... | collective-permute-start | bytes 184328 | tf_op jit(solution)/shard_map/ppermute | solution.py:30
  19.0 6.5 %collective-permute-start.5 = (f32[4,3840]{1,0:T(4,128)S(1)}, f32[4,3840]{1,0:T(4,128)S(1)}, u32[]{:S(2)}, u32[]{:S(2)}) collective-permute-start(f32[4,3840]{1,0:T(4,128)S(1)} %add.25), channel_id=1, source_target_pairs={{0,32},{32,0},{64,96},{96,64},{1,33},{33,1},{65,97},{97,65},{2,34}... | collective-permute-start | bytes 184328 | tf_op jit(solution)/shard_map/ppermute | solution.py:30
  20.3 5.2 %collective-permute-start.4 = (f32[4,3840]{1,0:T(4,128)S(1)}, f32[4,3840]{1,0:T(4,128)S(1)}, u32[]{:S(2)}, u32[]{:S(2)}) collective-permute-start(f32[4,3840]{1,0:T(4,128)S(1)} %add.25), channel_id=1, source_target_pairs={{0,24},{8,16},{16,8},{24,0},{1,25},{9,17},{17,9},{25,1},{2,26},{10... | collective-permute-start | bytes 184328 | tf_op jit(solution)/shard_map/ppermute | solution.py:30
  22.8 5.2 %collective-permute-start.3 = (f32[4,3840]{1,0:T(4,128)S(1)}, f32[4,3840]{1,0:T(4,128)S(1)}, u32[]{:S(2)}, u32[]{:S(2)}) collective-permute-start(f32[4,3840]{1,0:T(4,128)S(1)} %add.25), channel_id=1, source_target_pairs={{0,56},{8,48},{16,40},{24,32},{32,24},{40,16},{48,8},{56,0},{64,12... | collective-permute-start | bytes 184328 | tf_op jit(solution)/shard_map/ppermute | solution.py:30
  28.0 6.5 %collective-permute-start.8 = (f32[4,3840]{1,0:T(4,128)S(1)}, f32[4,3840]{1,0:T(4,128)S(1)}, u32[]{:S(2)}, u32[]{:S(2)}) collective-permute-start(f32[4,3840]{1,0:T(4,128)S(1)} %add_add_fusion.1), channel_id=1, source_target_pairs={{0,8},{8,0},{16,24},{24,16},{1,9},{9,1},{17,25},{25,17},{2,10},{10... | collective-permute-start | bytes 184328 | tf_op jit(solution)/shard_map/ppermute | solution.py:30
  28.1 6.4 %collective-permute-start.7 = (f32[4,3840]{1,0:T(4,128)S(1)}, f32[4,3840]{1,0:T(4,128)S(1)}, u32[]{:S(2)}, u32[]{:S(2)}) collective-permute-start(f32[4,3840]{1,0:T(4,128)S(1)} %add_add_fusion.1), channel_id=1, source_target_pairs={{0,96},{32,64},{64,32},{96,0},{1,97},{33,65},{65,33},{97,1},{2,98}... | collective-permute-start | bytes 184328 | tf_op jit(solution)/shard_map/ppermute | solution.py:30
  30.2 5.2 %collective-permute-start.6 = (f32[4,3840]{1,0:T(4,128)S(1)}, f32[4,3840]{1,0:T(4,128)S(1)}, u32[]{:S(2)}, u32[]{:S(2)}) collective-permute-start(f32[4,3840]{1,0:T(4,128)S(1)} %add_add_fusion.1), channel_id=1, source_target_pairs={{0,104},{8,96},{16,120},{24,112},{32,72},{40,64},{48,88},{56,80},{... | collective-permute-start | bytes 184328 | tf_op jit(solution)/shard_map/ppermute | solution.py:30
  35.5 5.6 %collective-permute-start.9 = (f32[4,3840]{1,0:T(4,128)S(1)}, f32[4,3840]{1,0:T(4,128)S(1)}, u32[]{:S(2)}, u32[]{:S(2)}) collective-permute-start(f32[4,3840]{1,0:T(4,128)S(1)} %add_add_fusion.refs_2_), channel_id=1, source_target_pairs={{0,4},{4,0},{1,5},{5,1},{2,6},{6,2},{3,7},{7,3},{8,12},{12,8},{9,1... | collective-permute-start | bytes 184328 | tf_op jit(solution)/shard_map/ppermute | solution.py:30
  42.2 4.1 %collective-permute-start.11 = (f32[48,112]{1,0:T(8,128)S(1)}, f32[48,112]{1,0:T(8,128)S(1)}, u32[]{:S(2)}, u32[]{:S(2)}) collective-permute-start(f32[48,112]{1,0:T(8,128)S(1)} %get-tuple-element.31), channel_id=1, source_target_pairs={{0,1},{1,0},{2,3},{3,2},{4,5},{5,4},{6,7},{7,6},{8,9},{9,8},{10,11... | collective-permute-start | bytes 64520 | tf_op jit(solution)/shard_map/ppermute | solution.py:30
  44.2 3.7 %collective-permute-start.12 = (f32[48,112]{1,0:T(8,128)S(1)}, f32[48,112]{1,0:T(8,128)S(1)}, u32[]{:S(2)}, u32[]{:S(2)}) collective-permute-start(f32[48,112]{1,0:T(8,128)S(1)} %get-tuple-element.32), channel_id=1, source_target_pairs={{0,2},{1,3},{2,0},{3,1},{4,6},{5,7},{6,4},{7,5},{8,10},{9,11},{10,... | collective-permute-start | bytes 64520 | tf_op jit(solution)/shard_map/ppermute | solution.py:30
  44.2 4.5 %collective-permute-start.13 = (f32[48,112]{1,0:T(8,128)S(1)}, f32[48,112]{1,0:T(8,128)S(1)}, u32[]{:S(2)}, u32[]{:S(2)}) collective-permute-start(f32[48,112]{1,0:T(8,128)S(1)} %get-tuple-element.33), channel_id=1, source_target_pairs={{0,3},{1,2},{2,1},{3,0},{4,7},{5,6},{6,5},{7,4},{8,11},{9,10},{10,... | collective-permute-start | bytes 64520 | tf_op jit(solution)/shard_map/ppermute | solution.py:30
